TPU v7x, 512 devices: a 8x2x16 block of a 8x8x16 slice. The times are simulated.
512 devices in a mesh: grp: 2 (over y), seq: 16 (over z), head: 8 (over x), sub: 2 (over core).
Axes of the slice: x: 8, y: 2, z: 16, core: 2. Of those that a mesh axis runs over, the one named last changes fastest.
The devices are a block of a 8x8x16 slice.
Arguments:
- vid_q: bfloat16 [10240, 4096], P(('grp', 'seq', 'sub'), 'head'), parts along dimension 0, may hold values from -6 to 6
- vid_k: bfloat16 [10240, 4096], P(('grp', 'seq', 'sub'), 'head'), parts along dimension 0, may hold values from -6 to 6
- vid_v: bfloat16 [10240, 4096], P(('grp', 'seq', 'sub'), 'head'), parts along dimension 0, may hold values from -6 to 6
- aud_q: bfloat16 [2560, 2048], P(('grp', 'seq', 'sub'), 'head'), parts along dimension 0, may hold values from -6 to 6
- cross_k: bfloat16 [10240, 2048], P(('grp', 'seq', 'sub'), 'head'), parts along dimension 0, may hold values from -6 to 6
- cross_v: bfloat16 [10240, 2048], P(('grp', 'seq', 'sub'), 'head'), parts along dimension 0, may hold values from -6 to 6
- cross_q: bfloat16 [10240, 2048], P(('grp', 'seq', 'sub'), 'head'), parts along dimension 0, may hold values from -6 to 6
- aud_k: bfloat16 [2560, 2048], P(('grp', 'seq', 'sub'), 'head'), parts along dimension 0, may hold values from -6 to 6
- aud_v: bfloat16 [2560, 2048], P(('grp', 'seq', 'sub'), 'head'), parts along dimension 0, may hold values from -6 to 6
- windows: int32 [2, 320], P(None, 'grp'), parts along dimension 1, may hold values from 0 to 160, as said below
Outputs:
- video_self: bfloat16 [10240, 4096], P(('grp', 'seq', 'sub'), 'head'), parts along dimension 0
- audio_out: bfloat16 [2560, 2048], P(('grp', 'seq', 'sub'), 'head'), parts along dimension 0
- video_cross: bfloat16 [10240, 2048], P(('grp', 'seq', 'sub'), 'head'), parts along dimension 0
There are 2 independent parts, one for each index of `grp`. A program takes and returns all parts, laid end to end along the dimension named above; each array names one. Nothing has to cross between parts.
Inputs may be any that keep to these rules, and one draw needn't show every extreme that they name: For every stretch c, windows[0, c] lies between max(0, c - 5) and c, and windows[1, c] between c + 1 and min(160, c + 6); in every draw some stretch reaches 5 tiles on both sides.
All inputs are finite; a program needn't handle non-finite values.
Results may differ from a plain program's by a relative error of at most 0.03.
Values may be sent and summed in bfloat16 or wider, within the bound.
No kernel may reach another device: no remote copies, remote signals or barrier semaphores. Data moves between devices by JAX's collectives and lax.ppermute only.
A program may use at most 64 MiB of HBM per device.

v0:
```python
from functools import partial
import math
import jax
import jax.numpy as jnp
from jax import lax
from jax.sharding import PartitionSpec as P

HEAD_DIM = 128
AUDIO_DIM = 64
TILE_LEN = 32
STRETCH_LEN = 8


def with_halo(array, sides, width):
    edges = {}
    for axis, dim in sides:
        count, length = (lax.axis_size(axis), array.shape[dim])
        up = [(i, (i + 1) % count) for i in range(count - 1)]
        last = lax.slice_in_dim(array, length - width, length, axis=dim)
        leading = lax.slice_in_dim(array, 0, width, axis=dim)
        edges[dim] = (
            lax.ppermute(last, axis, up),
            lax.ppermute(leading, axis, [(b, a) for a, b in up]),
        )
    done = []
    for _, dim in sides:
        low, high = edges[dim]
        around = [(width, width) if d in done else (0, 0) for d in range(array.ndim)]
        array = jnp.concatenate([jnp.pad(low, around), array, jnp.pad(high, around)], axis=dim)
        done.append(dim)
    return array


def start_state(query_count, head_count, head_size):
    running = jnp.full((head_count, query_count), -jnp.inf, jnp.float32)
    summed = jnp.zeros((head_count, query_count), jnp.float32)
    numerator = jnp.zeros((head_count, query_count, head_size), jnp.float32)
    return (running, summed, numerator)


def absorb(state_in, queries, key_rows, value_rows, head_count, scaling, visible):
    running, summed, numerator = state_in
    query_count = queries.shape[0]
    key_count = key_rows.shape[0]
    head_size = queries.shape[1] // head_count
    scores = (
        jnp.einsum(
            "qhe,khe->hqk",
            queries.reshape(query_count, head_count, head_size),
            key_rows.reshape(key_count, head_count, head_size),
            preferred_element_type=jnp.float32,
        )
        * scaling
    )
    if visible is not None:
        scores = jnp.where(visible[None], scores, jnp.float32(-1e30))
    newest = jnp.maximum(running, jnp.max(scores, axis=2))
    shrink = jnp.exp(running - newest)
    weights = jnp.exp(scores - newest[:, :, None])
    summed = summed * shrink + jnp.sum(weights, axis=2)
    numerator = numerator * shrink[:, :, None] + jnp.einsum(
        "hqk,khe->hqe",
        weights.astype(jnp.bfloat16),
        value_rows.reshape(key_count, head_count, head_size),
        preferred_element_type=jnp.float32,
    )
    return (newest, summed, numerator)


def block_split(total_rows):
    block_rows = total_rows
    while block_rows > 512 and block_rows % 2 == 0:
        block_rows = block_rows // 2
    return (block_rows, total_rows // block_rows)


def fold_joint(
    states_in,
    combined,
    offset,
    video_queries,
    audio_queries,
    video_heads,
    audio_heads,
    video_scaling,
    audio_scaling,
):
    video_width = video_queries.shape[1]
    audio_width = audio_queries.shape[1]
    block_rows, block_count = block_split(combined.shape[0])
    blocks = combined.reshape(block_count, block_rows, combined.shape[1])

    def one_block(states, rows):
        video_state = absorb(
            states[0],
            video_queries,
            rows[:, :video_width],
            rows[:, video_width : 2 * video_width],
            video_heads,
            video_scaling,
            None,
        )
        audio_state = absorb(
            states[1],
            audio_queries,
            rows[:, 2 * video_width : 2 * video_width + audio_width],
            rows[:, 2 * video_width + audio_width :],
            audio_heads,
            audio_scaling,
            None,
        )
        return ((video_state, audio_state), None)

    result, unused = lax.scan(one_block, states_in, blocks)
    return result


def normalize_heads(state_in):
    running, summed, numerator = state_in
    mixed = numerator / summed[:, :, None]
    return mixed.transpose(1, 0, 2).reshape(mixed.shape[1], -1).astype(jnp.bfloat16)


def body(vid_q, vid_k, vid_v, aud_q, cross_k, cross_v, cross_q, aud_k, aud_v, windows):
    video_heads = vid_q.shape[1] // HEAD_DIM
    video_scaling = 1.0 / math.sqrt(HEAD_DIM)
    audio_heads = aud_q.shape[1] // AUDIO_DIM
    audio_scaling = 1.0 / math.sqrt(AUDIO_DIM)
    combined = jnp.concatenate((vid_k, vid_v, cross_k, cross_v), axis=1)
    folder = partial(
        fold_joint,
        video_queries=vid_q,
        audio_queries=aud_q,
        video_heads=video_heads,
        audio_heads=audio_heads,
        video_scaling=video_scaling,
        audio_scaling=audio_scaling,
    )
    initial = (
        start_state(vid_q.shape[0], video_heads, HEAD_DIM),
        start_state(aud_q.shape[0], audio_heads, AUDIO_DIM),
    )
    video_state, audio_state = folder(
        initial, lax.all_gather(combined, ("seq", "sub"), axis=0, tiled=True), jnp.int32(0)
    )
    video_self = normalize_heads(video_state)
    audio_out = normalize_heads(audio_state)
    audio_rows = aud_k.shape[0]
    key_width = aud_k.shape[1]
    padded_rows = with_halo(
        jnp.concatenate((aud_k, aud_v), axis=1), ((("seq", "sub"), 0),), audio_rows
    )
    near_keys = padded_rows[:, :key_width]
    near_values = padded_rows[:, key_width:]
    position = lax.axis_index(("seq", "sub"))
    audio_index = (position - 1) * audio_rows + jnp.arange(padded_rows.shape[0], dtype=jnp.int32)
    stretch_index = audio_index // STRETCH_LEN
    stretch_ids = jnp.arange(windows.shape[1], dtype=jnp.int32)
    onehot = stretch_index[:, None] == stretch_ids[None, :]
    first_tile = jnp.sum(jnp.where(onehot, windows[0][None, :], 0), axis=1)
    after_tile = jnp.sum(jnp.where(onehot, windows[1][None, :], 0), axis=1)
    video_rows = cross_q.shape[0]
    video_tile = (position * video_rows + jnp.arange(video_rows, dtype=jnp.int32)) // TILE_LEN
    visible = (first_tile[None, :] <= video_tile[:, None]) & (
        video_tile[:, None] < after_tile[None, :]
    )
    state = absorb(
        start_state(video_rows, audio_heads, AUDIO_DIM),
        cross_q,
        near_keys,
        near_values,
        audio_heads,
        audio_scaling,
        visible,
    )
    video_cross = normalize_heads(state)
    return (video_self, audio_out, video_cross)


def solution(mesh):
    return jax.shard_map(
        body,
        mesh=mesh,
        in_specs=(
            P(("grp", "seq", "sub"), "head"),
            P(("grp", "seq", "sub"), "head"),
            P(("grp", "seq", "sub"), "head"),
            P(("grp", "seq", "sub"), "head"),
            P(("grp", "seq", "sub"), "head"),
            P(("grp", "seq", "sub"), "head"),
            P(("grp", "seq", "sub"), "head"),
            P(("grp", "seq", "sub"), "head"),
            P(("grp", "seq", "sub"), "head"),
            P(None, "grp"),
        ),
        out_specs=(
            P(("grp", "seq", "sub"), "head"),
            P(("grp", "seq", "sub"), "head"),
            P(("grp", "seq", "sub"), "head"),
        ),
        check_vma=False,
    )
```

profile of v0, /device:TPU:65, one launch (start us, length us, event | category | flops | bytes accessed | tf_op | source)
XLA Modules:
  0.0 245.9 jit_solution(11769549434553629268)
XLA Ops:
  7.2 1.9 pad_maximum_fusion
  10.7 7.0 %collective-permute-start = (bf16[40,512]{1,0:T(8,128)(2,1)S(1)}, bf16[40,512]{1,0:T(8,128)(2,1)S(1)}, u32[]{:S(2)}, u32[]{:S(2)}) collective-permute-start(bf16[40,512]{1,0:T(8,128)(2,1)S(1)} %constant_dynamic-update-slice_fusion), channel_id=1, source_target_pairs={{0,1},{1,16},{16,17},{17,32},{32,33},{33,48},{48,49},{49,64},{64,6... | collective-permute-start | bytes 122888 | tf_op jit(solution)/shard_map/ppermute | solution.py:22
  17.7 37.6 %collective-permute-start.1 = (bf16[40,512]{1,0:T(8,128)(2,1)S(1)}, bf16[40,512]{1,0:T(8,128)(2,1)S(1)}, u32[]{:S(2)}, u32[]{:S(2)}) collective-permute-start(bf16[40,512]{1,0:T(8,128)(2,1)S(1)} %constant_dynamic-update-slice_fusion), channel_id=1, source_target_pairs={{1,0},{16,1},{17,16},{32,17},{33,32},{48,33},{49,48},{64,49},{65,6... | collective-permute-start | bytes 122888 | tf_op jit(solution)/shard_map/ppermute | solution.py:23
  59.6 89.6 %all-gather.2.cloned.1.call-done = bf16[5120,1536]{1,0:T(8,128)(2,1)} async-done(((bf16[160,1536]{1,0:T(8,128)(2,1)}), bf16[5120,1536]{1,0:T(8,128)(2,1)}) %all-gather.2.cloned.1.call-update) | async-done | bytes 15728656 | tf_op jit(solution)/shard_map/all_gather | solution.py:144
  149.2 88.1 %while.21 = (s32[]{:T(128)}, f32[4,160]{1,0:T(4,128)S(1)}, f32[4,160]{1,0:T(4,128)S(1)}, f32[4,160,128]{2,1,0:T(8,128)S(1)}, f32[4,40]{1,0:T(4,128)S(1)}, /*inde...) while((s32[]{:T(128)}, f32[4,160]{1,0:T(4,128)S(1)}, ...), condition=%wide.region_5.6_spmd.clone, body=%wide.region_0.5_spmd.clone.sunk | while | flops 119781280 | bytes 9656456 | solution.py:114
  152.5 1.3 fusion.62
  154.7 1.3 dynamic-slice_bitcast_fusion.2
  158.0 1.3 fusion.62
  160.2 1.3 dynamic-slice_bitcast_fusion.2
  163.5 1.3 fusion.62
  165.7 1.3 dynamic-slice_bitcast_fusion.2
  169.0 1.3 fusion.62
  171.3 1.3 dynamic-slice_bitcast_fusion.2
  174.5 1.3 fusion.62
  176.8 1.3 dynamic-slice_bitcast_fusion.2
  180.0 1.3 fusion.62
  182.3 1.3 dynamic-slice_bitcast_fusion.2
  185.6 1.3 fusion.62
  187.8 1.3 dynamic-slice_bitcast_fusion.2
  191.1 1.3 fusion.62
  193.3 1.3 dynamic-slice_bitcast_fusion.2
  196.6 1.3 fusion.62
  202.1 1.3 fusion.62
  207.6 1.3 fusion.62
  213.1 1.3 fusion.62
  218.6 1.3 fusion.62
  220.8 1.3 dynamic-slice_bitcast_fusion.2
  224.1 1.3 fusion.62
  226.3 1.3 dynamic-slice_bitcast_fusion.2
  229.6 1.3 fusion.62
  231.8 1.3 dynamic-slice_bitcast_fusion.2
  235.1 1.3 fusion.62
  (293 shorter events, 58.9 us)
Async XLA Ops:
  7.2 142.0 %all-gather.2.cloned.1.call-start = ((), (), s32[]{:S(2)}) async-start(), calls=%async_computation | async-start | bytes 16220160 | tf_op jit(solution)/shard_map/all_gather | solution.py:144
  10.7 46.8 %collective-permute-start = (bf16[40,512]{1,0:T(8,128)(2,1)S(1)}, bf16[40,512]{1,0:T(8,128)(2,1)S(1)}, u32[]{:S(2)}, u32[]{:S(2)}) collective-permute-start(bf16[40,512]{1,0:T(8,128)(2,1)S(1)} %constant_dynamic-update-slice_fusion), channel_id=1, source_target_pairs={{0,1},{1,16},{16,17},{17,32},{32,33},{33,48},{48,49},{49,64},{64,6... | collective-permute-start | bytes 122888 | tf_op jit(solution)/shard_map/ppermute | solution.py:22
  17.7 39.7 %collective-permute-start.1 = (bf16[40,512]{1,0:T(8,128)(2,1)S(1)}, bf16[40,512]{1,0:T(8,128)(2,1)S(1)}, u32[]{:S(2)}, u32[]{:S(2)}) collective-permute-start(bf16[40,512]{1,0:T(8,128)(2,1)S(1)} %constant_dynamic-update-slice_fusion), channel_id=1, source_target_pairs={{1,0},{16,1},{17,16},{32,17},{33,32},{48,33},{49,48},{64,49},{65,6... | collective-permute-start | bytes 122888 | tf_op jit(solution)/shard_map/ppermute | solution.py:23
Sparse Core Ops, SparseCore 0:
  10.1 139.0 all-gather.1
where the time goes:
time: 248 us; the launch traced here: 246 us
  waiting for transfers between devices  89.7 us (36%)
  local copies, waits for them, and re-layouts  44.9 us (18%)
  starting transfers between devices  44.7 us (18%)
  matrix products  36.4 us (15%)
  other arithmetic  14.5 us (6%)
  between operations  14.2 us (6%)
    all_gather x1, waiting for transfers between devices, body(): lax.all_gather(combined, ('seq', 'sub'), axis=0, tiled=True)  89.6 us
    ppermute x1, starting transfers between devices, with_halo(): lax.ppermute(leading, axis, [(b, a) for a, b in up])  37.6 us
    dot_general x33, matrix products, absorb(): jnp.einsum('qhe,khe->hqk', queries.reshape(query_count, head_count, head_...  25.7 us
    squeeze x16, local copies, waits for them, and re-layouts, fold_joint(): result, unused = lax.scan(one_block, states_in, blocks)  20.3 us
    reshape x16, local copies, waits for them, and re-layouts, absorb(): queries.reshape(query_count, head_count, head_size)  13.2 us
    dot_general x33, matrix products, absorb(): jnp.einsum('hqk,khe->hqe', weights.astype(jnp.bfloat16), value_rows.resha...  10.7 us
    reduce_sum x33, other arithmetic, absorb(): summed = summed * shrink + jnp.sum(weights, axis=2)  10.7 us
    ppermute x1, starting transfers between devices, with_halo(): lax.ppermute(last, axis, up)  7.05 us
  transfers between devices with their start and end apart: 3, of which 1 were waited for; matrix products, arithmetic and copies ran while one was open for 2% of the time, Pallas kernels for 0%

commit v1 on v0

--- a/solution.py
+++ b/solution.py
@@ -141,7 +141,14 @@
         start_state(aud_q.shape[0], audio_heads, AUDIO_DIM),
     )
     video_state, audio_state = folder(
-        initial, lax.all_gather(combined, ("seq", "sub"), axis=0, tiled=True), jnp.int32(0)
+        initial,
+        jnp.concatenate(
+            lax.all_to_all(
+                jnp.stack([combined] * lax.axis_size(("seq", "sub"))), ("seq", "sub"), 0, 0
+            ),
+            axis=0,
+        ),
+        jnp.int32(0),
     )
     video_self = normalize_heads(video_state)
     audio_out = normalize_heads(audio_state)

time: 248 us -> 801 us (3.23)
  waiting for transfers between devices: 89.7 us -> 669 us
  matrix products: 36.4 us -> 21.8 us
  between operations: 14.2 us -> 0.89 us
  local copies, waits for them, and re-layouts: 44.9 us -> 35.8 us
    ppermute x1, waiting for transfers between devices: 0.01 us -> 649 us  [with_halo(): lax.ppermute(last, axis, up)]
    all_gather x1 -> x0, waiting for transfers between devices: 89.6 us -> none  [body(): lax.all_gather(combined, ('seq', 'sub'), axis=0, tiled=True)]
    all_to_all x0 -> x1, starting transfers between devices: none -> 46.5 us  [body(): lax.all_to_all(jnp.stack([combined] * lax.axis_size(('seq', 'sub'))), ('s...]
    ppermute x1, starting transfers between devices: 37.6 us -> 1.95 us  [with_halo(): lax.ppermute(leading, axis, [(b, a) for a, b in up])]
    ppermute x1, waiting for transfers between devices: 0.01 us -> 20.4 us  [with_halo(): lax.ppermute(leading, axis, [(b, a) for a, b in up])]
    dot_general x33, matrix products: 25.7 us -> 11.1 us  [absorb(): jnp.einsum('qhe,khe->hqk', queries.reshape(query_count, head_count, head_...]
    reshape x16, local copies, waits for them, and re-layouts: 13.2 us -> 1.5 us  [absorb(): queries.reshape(query_count, head_count, head_size)]
  transfers between devices with their start and end apart: 3 -> 3, of which waited for: 1 -> 2; matrix products, arithmetic and copies ran while one was open for 2% -> 0% of each run, Pallas kernels for 0% -> 0%
where the time goes in v1:
time: 801 us; the launch traced here: 795 us
  waiting for transfers between devices  669 us (84%)
  starting transfers between devices  52 us (6%)
  local copies, waits for them, and re-layouts  35.8 us (4%)
  matrix products  21.8 us (3%)
  other arithmetic  13.8 us (2%)
    ppermute x1, waiting for transfers between devices, with_halo(): lax.ppermute(last, axis, up)  649 us
    all_to_all x1, starting transfers between devices, body(): lax.all_to_all(jnp.stack([combined] * lax.axis_size(('seq', 'sub'))), ('s...  46.5 us
    ppermute x1, waiting for transfers between devices, with_halo(): lax.ppermute(leading, axis, [(b, a) for a, b in up])  20.4 us
    squeeze x16, local copies, waits for them, and re-layouts, fold_joint(): result, unused = lax.scan(one_block, states_in, blocks)  20.3 us
  transfers between devices with their start and end apart: 3, of which 2 were waited for; matrix products, arithmetic and copies ran while one was open for 0% of the time, Pallas kernels for 0%

profile of v1, /device:TPU:65, one launch (start us, length us, event | category | flops | bytes accessed | tf_op | source)
XLA Modules:
  0.0 795.1 jit_solution(2064035296084082592)
XLA Ops:
  0.6 1.1 pad_maximum_fusion
  1.7 5.7 stack.2
  7.5 46.5 %all-to-all-start = ((bf16[32,160,1536]{2,1,0:T(8,128)(2,1)}), bf16[32,160,1536]{2,1,0:T(8,128)(2,1)}, u32[]{:S(2)}, u32[]{:S(2)}) async-start(bf16[32,160,1536]{2,1,0:T(8,128)(2,1)} %stack.2), calls=%async_computation | async-start | bytes 31457280 | tf_op jit(solution)/shard_map/all_to_all | solution.py:146
  54.0 3.6 collective-permute-start
  57.6 2.0 collective-permute-start.1
  60.0 649.0 %collective-permute-done = bf16[40,512]{1,0:T(8,128)(2,1)S(1)} collective-permute-done((bf16[40,512]{1,0:T(8,128)(2,1)S(1)}, bf16[40,512]{1,0:T(8,128)(2,1)S(1)}, u32[]{:S(2)}, u32[]{:S(2)}) %collective-permute-start) | collective-permute-done | bytes 40992 | tf_op jit(solution)/shard_map/ppermute | solution.py:22
  709.0 20.4 %collective-permute-done.1 = bf16[40,512]{1,0:T(8,128)(2,1)S(1)} collective-permute-done((bf16[40,512]{1,0:T(8,128)(2,1)S(1)}, bf16[40,512]{1,0:T(8,128)(2,1)S(1)}, u32[]{:S(2)}, u32[]{:S(2)}) %collective-permute-start.1) | collective-permute-done | bytes 40992 | tf_op jit(solution)/shard_map/ppermute | solution.py:23
  730.9 0.7 copy.44
  731.6 61.8 %while.21 = (s32[]{:T(128)}, f32[4,160]{1,0:T(4,128)S(1)}, f32[4,160]{1,0:T(4,128)S(1)}, f32[4,160,128]{2,1,0:T(8,128)S(1)}, f32[4,40]{1,0:T(4,128)S(1)}, /*inde...) while((s32[]{:T(128)}, f32[4,160]{1,0:T(4,128)S(1)}, ...), condition=%wide.region_5.6_spmd.clone, body=%wide.region_0.5_spmd.clone.sunk | while | flops 119781280 | bytes 9656456 | solution.py:114
  731.6 1.3 dynamic-slice_bitcast_fusion.2
  734.6 0.4 fusion.63
  735.5 1.3 dynamic-slice_bitcast_fusion.2
  738.5 0.4 fusion.63
  739.4 1.3 dynamic-slice_bitcast_fusion.2
  742.3 0.4 fusion.63
  743.2 1.3 dynamic-slice_bitcast_fusion.2
  747.1 1.3 dynamic-slice_bitcast_fusion.2
  751.0 1.3 dynamic-slice_bitcast_fusion.2
  754.8 1.3 dynamic-slice_bitcast_fusion.2
  757.8 0.4 fusion.63
  758.7 1.3 dynamic-slice_bitcast_fusion.2
  761.7 0.4 fusion.63
  762.6 1.3 dynamic-slice_bitcast_fusion.2
  766.4 1.3 dynamic-slice_bitcast_fusion.2
  770.3 1.3 dynamic-slice_bitcast_fusion.2
  774.2 1.3 dynamic-slice_bitcast_fusion.2
  778.0 1.3 dynamic-slice_bitcast_fusion.2
  781.9 1.3 dynamic-slice_bitcast_fusion.2
  785.8 1.3 dynamic-slice_bitcast_fusion.2
  789.6 1.3 dynamic-slice_bitcast_fusion.2
  793.6 0.7 convert_element_type.38
  794.3 0.8 copy_bitcast_fusion
  (305 shorter events, 39.8 us)
Async XLA Ops:
  7.4 46.5 %copy-start.3 = (bf16[40,256]{1,0:T(8,128)(2,1)S(1)}, bf16[40,256]{1,0:T(8,128)(2,1)}, u32[]{:S(2)}) copy-start(bf16[40,256]{1,0:T(8,128)(2,1)} %param.19) | copy-start | bytes 61444
  7.4 46.5 %copy-start.4 = (bf16[40,256]{1,0:T(8,128)(2,1)S(1)}, bf16[40,256]{1,0:T(8,128)(2,1)}, u32[]{:S(2)}) copy-start(bf16[40,256]{1,0:T(8,128)(2,1)} %param.20) | copy-start | bytes 61444
  7.4 52.2 %copy-start.5 = (s32[2,160]{1,0:T(2,128)S(1)}, s32[2,160]{1,0:T(2,128)}, u32[]{:S(2)}) copy-start(s32[2,160]{1,0:T(2,128)} %param.21) | copy-start | bytes 3844
  7.5 52.5 %copy-start.2 = (bf16[160,256]{1,0:T(8,128)(2,1)S(1)}, bf16[160,256]{1,0:T(8,128)(2,1)}, u32[]{:S(2)}) copy-start(bf16[160,256]{1,0:T(8,128)(2,1)} %param.18) | copy-start | bytes 245764
  7.5 724.2 %copy-start = (bf16[160,512]{1,0:T(8,128)(2,1)S(1)}, bf16[160,512]{1,0:T(8,128)(2,1)}, u32[]{:S(2)}) copy-start(bf16[160,512]{1,0:T(8,128)(2,1)} %param.12) | copy-start | bytes 491524
  7.5 724.2 %copy-start.1 = (bf16[40,256]{1,0:T(8,128)(2,1)S(1)}, bf16[40,256]{1,0:T(8,128)(2,1)}, u32[]{:S(2)}) copy-start(bf16[40,256]{1,0:T(8,128)(2,1)} %param.15) | copy-start | bytes 61444
  7.5 724.1 %all-to-all-start = ((bf16[32,160,1536]{2,1,0:T(8,128)(2,1)}), bf16[32,160,1536]{2,1,0:T(8,128)(2,1)}, u32[]{:S(2)}, u32[]{:S(2)}) async-start(bf16[32,160,1536]{2,1,0:T(8,128)(2,1)} %stack.2), calls=%async_computation | async-start | bytes 31457280 | tf_op jit(solution)/shard_map/all_to_all | solution.py:146
  54.0 655.0 %collective-permute-start = (bf16[40,512]{1,0:T(8,128)(2,1)S(1)}, bf16[40,512]{1,0:T(8,128)(2,1)S(1)}, u32[]{:S(2)}, u32[]{:S(2)}) collective-permute-start(bf16[40,512]{1,0:T(8,128)(2,1)S(1)} %constant_dynamic-update-slice_fusion), channel_id=1, source_target_pairs={{0,1},{1,16},{16,17},{17,32},{32,33},{33,48},{48,49},{49,64},{64,6... | collective-permute-start | bytes 122888 | tf_op jit(solution)/shard_map/ppermute | solution.py:22
  57.6 671.8 %collective-permute-start.1 = (bf16[40,512]{1,0:T(8,128)(2,1)S(1)}, bf16[40,512]{1,0:T(8,128)(2,1)S(1)}, u32[]{:S(2)}, u32[]{:S(2)}) collective-permute-start(bf16[40,512]{1,0:T(8,128)(2,1)S(1)} %constant_dynamic-update-slice_fusion), channel_id=1, source_target_pairs={{1,0},{16,1},{17,16},{32,17},{33,32},{48,33},{49,48},{64,49},{65,6... | collective-permute-start | bytes 122888 | tf_op jit(solution)/shard_map/ppermute | solution.py:23
